TPU v7x, 32 devices: a whole 2x2x4 slice. The times are simulated.
32 devices in a mesh: seq: 8 (over z, y), ch: 4 (over x, core).
Axes of the slice: x: 2, y: 2, z: 4, core: 2. Of those that a mesh axis runs over, the one named last changes fastest.
Arguments:
- signal: float32 [1, 65536, 1024], P(None, 'seq', 'ch'), may hold values from -6 to 6
- spectrum: float32 [2, 256, 256, 1024], P(None, 'seq', None, 'ch'), may hold values from -6 to 6
- channel_mode: int32 [1024], P('ch'), may hold values 0 or 1
- skip_gain: float32 [1024], P('ch'), may hold values from -4 to 4
- out_weight: bfloat16 [1024, 1024], P('ch'), may hold values from -0.1875 to 0.1875
Outputs:
- projected: float32 [1, 65536, 1024], P(None, 'seq', 'ch')
Inputs may be any that keep to these rules, and one draw needn't show every extreme that they name: `channel_mode`: 1 marks a channel whose 65536 positions are one sequence, 0 a channel whose positions form a 256 x 256 image.
All inputs are finite; a program needn't handle non-finite values. No bound on the sum of `channel_mode` on one device may be relied on, other than what follows from the above.
Results may differ from a plain program's by a relative error of at most 0.017.
Values may be sent and summed in bfloat16 or wider, within the bound.
A program may use at most 192 MiB of HBM per device.

v0:
```python
import math

import jax
import jax.numpy as jnp
from jax import lax
from jax.sharding import PartitionSpec as P

ROWS = 256
COLUMNS = 256
LENGTH = 65536


def contract(pattern, operand, matrix):
    return jnp.einsum(
        pattern,
        operand,
        matrix,
        precision=lax.Precision.HIGHEST,
        preferred_element_type=jnp.float32,
    )


def phase_table(row_index, col_index, period):
    product = row_index[:, None] * col_index[None, :] % period
    angles = product.astype(jnp.float32) * (2.0 * math.pi / period)
    return (jnp.cos(angles), jnp.sin(angles))


def square_table(length):
    counter = jnp.arange(length, dtype=jnp.int32)
    return phase_table(counter, counter, length)


def transform_real(pattern, operand, cosine_table, sine_table):
    return (contract(pattern, operand, cosine_table), -contract(pattern, operand, sine_table))


def transform_complex(pattern, real_part, imag_part, cosine_table, sine_table, orient):
    real_out = contract(pattern, real_part, cosine_table) - orient * contract(
        pattern, imag_part, sine_table
    )
    imag_out = orient * contract(pattern, real_part, sine_table) + contract(
        pattern, imag_part, cosine_table
    )
    return (real_out, imag_out)


def inverse_real(pattern, real_part, imag_part, cosine_table, sine_table, factor):
    return (
        contract(pattern, real_part, cosine_table) - contract(pattern, imag_part, sine_table)
    ) * factor


def rotate(real_part, imag_part, cosine_table, sine_table, orient):
    real_out = real_part * cosine_table - orient * imag_part * sine_table
    imag_out = orient * real_part * sine_table + imag_part * cosine_table
    return (real_out, imag_out)


def filter_product(real_part, imag_part, filter_real, filter_imag):
    return (
        real_part * filter_real - imag_part * filter_imag,
        real_part * filter_imag + imag_part * filter_real,
    )


def channel_plan(signal, spectrum, channel_mode):
    groups = lax.axis_size("seq")
    position = lax.axis_index("seq")
    batches, local_len, owned = signal.shape
    rows_local = ROWS // groups
    shared = owned // groups
    tiled = signal.reshape(batches, rows_local, COLUMNS, owned)
    gathered, filters = (
        lax.all_to_all(
            tiled.astype(jnp.bfloat16), "seq", split_axis=3, concat_axis=1, tiled=True
        ).astype(tiled.dtype),
        lax.all_to_all(
            spectrum.astype(jnp.bfloat16), "seq", split_axis=3, concat_axis=1, tiled=True
        ).astype(spectrum.dtype),
    )
    own_modes = lax.dynamic_slice_in_dim(channel_mode, position * shared, shared)
    selector = (own_modes == 1)[None, :, None, None]
    images = jnp.transpose(gathered, (0, 3, 1, 2))
    filters_first = jnp.transpose(filters, (0, 3, 1, 2))
    row_cos, row_sin = square_table(ROWS)
    col_cos, col_sin = square_table(COLUMNS)
    twist_cos, twist_sin = phase_table(
        jnp.arange(ROWS, dtype=jnp.int32), jnp.arange(COLUMNS, dtype=jnp.int32), LENGTH
    )
    chosen_cos = jnp.where(selector, twist_cos[None, None], 1.0)
    chosen_sin = jnp.where(selector, twist_sin[None, None], 0.0)
    real_part, imag_part = transform_real("xmab,ad->xmdb", images, row_cos, row_sin)
    real_part, imag_part = rotate(real_part, imag_part, chosen_cos, chosen_sin, -1.0)
    real_part, imag_part = transform_complex(
        "xmdb,bc->xmdc", real_part, imag_part, col_cos, col_sin, -1.0
    )
    real_part, imag_part = filter_product(
        real_part, imag_part, filters_first[0][None], filters_first[1][None]
    )
    real_part, imag_part = transform_complex(
        "xmdc,cb->xmdb", real_part, imag_part, col_cos, col_sin, 1.0
    )
    real_part, imag_part = rotate(real_part, imag_part, chosen_cos, chosen_sin, 1.0)
    convolved = inverse_real("xmdb,da->xmab", real_part, imag_part, row_cos, row_sin, 1.0 / LENGTH)
    convolved = jnp.transpose(convolved, (0, 2, 3, 1))
    restored = lax.all_to_all(
        convolved.astype(jnp.bfloat16), "seq", split_axis=1, concat_axis=3, tiled=True
    ).astype(convolved.dtype)
    return restored.reshape(batches, local_len, owned)


def per_device(signal, spectrum, channel_mode, skip_gain, out_weight):
    convolved = channel_plan(signal, spectrum, channel_mode)
    hidden = (convolved + skip_gain[None, None, :] * signal).astype(jnp.bfloat16)
    partials = jnp.einsum("xtc,cj->xtj", hidden, out_weight, preferred_element_type=jnp.float32)
    return lax.psum_scatter(
        partials.astype(jnp.bfloat16), "ch", scatter_dimension=2, tiled=True
    ).astype(jnp.float32)


def solution(mesh):
    placed = (P(None, "seq", "ch"), P(None, "seq", None, "ch"), P("ch"), P("ch"), P("ch", None))
    return jax.shard_map(
        per_device, mesh=mesh, in_specs=placed, out_specs=P(None, "seq", "ch"), check_vma=False
    )
```

profile of v0, /device:TPU:0, one launch (start us, length us, event | category | flops | bytes accessed | tf_op | source)
XLA Modules:
  0.0 736.7 jit_solution(1022630028297481340)
XLA Ops:
  12.4 7.9 %copy.55 = bf16[1,32,256,256]{2,1,0,3:T(8,128)(2,1)} copy(bf16[1,32,256,256]{3,2,1,0:T(8,128)(2,1)} %bitcast.140) | data formatting | bytes 8388608 | tf_op jit(solution)/shard_map/convert_element_type | solution.py:76
  20.3 7.3 all-to-all-start
  27.6 16.8 %copy.62 = bf16[2,32,256,256]{2,1,0,3:T(8,128)(2,1)} copy(f32[2,32,256,256]{3,2,1,0:T(8,128)} %param.6) | data formatting | bytes 25165824 | tf_op args[1]
  44.5 76.5 %all-to-all-done = bf16[1,32,256,256]{2,1,0,3:T(8,128)(2,1)} async-done(((bf16[1,32,256,256]{2,1,0,3:T(8,128)(2,1)}), bf16[1,32,256,256]{2,1,0,3:T(8,128)(2,1)}, u32[]{:S(2)}, u32[]{:S(2)}) %all-to-all-start) | async-done | bytes 4194336 | tf_op jit(solution)/shard_map/all_to_all | solution.py:75
  145.0 11.7 %fusion.55 = f32[32,256,256]{2,1,0:T(8,128)} fusion(f32[256,32,256]{2,0,1:T(8,128)S(1)} %fusion.58, f32[256,32,256]{2,0,1:T(8,128)S(1)} %fusion.50, f32[256,256]{1,0:T(8,128)S(1)} %copy.59, f32[256,256]{1,0:T(8,128)S(1)} %copy.58, pred[32]{0:T(512)(128)(4,1)S(1)} %dynamic-slice_compare_fusion), kind=kOutput, calls=%fused_computation.76 | convolution fusion | flops 6458048512 | bytes 25690144 | tf_op jit(solution)/shard_map/xmdb,bc->xmdc/dot_general | solution.py:14
  156.7 12.0 %fusion.46 = f32[32,256,256]{2,1,0:T(8,128)} fusion(f32[256,32,256]{2,0,1:T(8,128)S(1)} %fusion.58, f32[256,32,256]{2,0,1:T(8,128)S(1)} %fusion.50, f32[256,256]{1,0:T(8,128)S(1)} %copy.59, f32[256,256]{1,0:T(8,128)S(1)} %copy.58, pred[32]{0:T(512)(128)(4,1)S(1)} %dynamic-slice_compare_fusion), kind=kOutput, calls=%fused_computation.67 | convolution fusion | flops 6458048512 | bytes 25690144 | tf_op jit(solution)/shard_map/xmdb,bc->xmdc/dot_general | solution.py:14
  168.6 14.4 %multiply_subtract_fusion = f32[32,256,256]{2,1,0:T(8,128)} fusion(f32[32,256,256]{2,1,0:T(8,128)} %fusion.55, f32[256,32,256]{2,0,1:T(8,128)S(1)} %fusion.58, f32[256,32,256]{2,0,1:T(8,128)S(1)} %fusion.50, f32[256,256]{1,0:T(8,128)S(1)} %copy.59, f32[256,256]{1,0:T(8,128)S(1)} %copy.58, pred[32]{0:T(512)(128)(4,1)S(1)} %dynamic-slice_compare_fusion), kind=kOutput, calls=%fused_computation.38 | convolution fusion | flops 6462242816 | bytes 34078752 | tf_op jit(solution)/shard_map/xmdb,bc->xmdc/dot_general | solution.py:14
  183.0 125.1 %all-to-all-done.1 = bf16[2,32,256,256]{2,1,0,3:T(8,128)(2,1)} async-done(((bf16[2,32,256,256]{2,1,0,3:T(8,128)(2,1)}), bf16[2,32,256,256]{2,1,0,3:T(8,128)(2,1)}, u32[]{:S(2)}, u32[]{:S(2)}) %all-to-all-start.1) | async-done | bytes 8388640 | tf_op jit(solution)/shard_map/all_to_all | solution.py:78
  308.1 11.4 %copy.63 = bf16[2,32,256,256]{2,3,1,0:T(8,128)(2,1)} copy(bf16[2,32,256,256]{2,1,0,3:T(8,128)(2,1)} %all-to-all-done.1) | data formatting | bytes 16777216 | tf_op jit(solution)/shard_map/all_to_all | solution.py:78
  319.5 11.4 %convert_bitcast_fusion = f32[2,8,32,256,32]{3,4,1,2,0:T(8,128)} fusion(bf16[2,32,256,8,32]{2,4,3,1,0:T(8,128)(2,1)} %bitcast.138), kind=kLoop, calls=%fused_computation | loop fusion | flops 4194304 | bytes 25165824 | tf_op jit(solution)/shard_map/transpose | solution.py:85
  330.9 17.8 %copy.64 = f32[2,8,32,256,32]{3,2,1,4,0:T(8,128)} copy(f32[2,8,32,256,32]{3,4,1,2,0:T(8,128)} %convert_bitcast_fusion) | data formatting | bytes 33554432 | tf_op jit(solution)/shard_map/transpose | solution.py:85
  348.7 27.1 %fusion.19 = (f32[1,32,256,256]{3,2,1,0:T(8,128)}, f32[1,32,256,256]{3,2,1,0:T(8,128)}) fusion(f32[32,256,256]{2,1,0:T(8,128)} %multiply_subtract_fusion, f32[2,32,256,256]{3,2,1,0:T(8,128)} %bitcast.137, f32[256,32,256]{2,0,1:T(8,128)} %copy-done.1, f32[256,32,256]{2,0,1:T(8,128)} %copy-done.2, f32[256,256]{1,0:T(8,128)S(1)} %copy.59, ...), kind=kOutput, calls=%fused_computation.29 | convolution fusion | flops 6474825728 | bytes 67633184 | tf_op jit(solution)/shard_map/xmdb,bc->xmdc/dot_general | solution.py:14
  375.8 13.2 %fusion.14 = f32[32,256,256]{2,1,0:T(8,128)} fusion(f32[1,32,256,256]{3,2,1,0:T(8,128)} %get-tuple-element.6), kind=kOutput, calls=%fused_computation.22 | convolution fusion | flops 6443368448 | bytes 16777216 | tf_op jit(solution)/shard_map/xmdc,cb->xmdb/dot_general | solution.py:14
  389.0 11.2 %fusion.16 = f32[32,256,256]{2,1,0:T(8,128)} fusion(f32[1,32,256,256]{3,2,1,0:T(8,128)S(1)} %copy-done.3), kind=kOutput, calls=%fused_computation.24 | convolution fusion | flops 6443368448 | bytes 16777216 | tf_op jit(solution)/shard_map/xmdc,cb->xmdb/dot_general | solution.py:14
  400.1 10.8 %fusion.10 = f32[32,256,256]{2,1,0:T(8,128)} fusion(f32[1,32,256,256]{3,2,1,0:T(8,128)S(1)} %bitcast.134), kind=kOutput, calls=%fused_computation.18 | convolution fusion | flops 6443368448 | bytes 16777216 | tf_op jit(solution)/shard_map/xmdc,cb->xmdb/dot_general | solution.py:14
  411.0 11.0 %fusion.12 = f32[32,256,256]{2,1,0:T(8,128)} fusion(f32[1,32,256,256]{3,2,1,0:T(8,128)S(1)} %bitcast.134), kind=kOutput, calls=%fused_computation.20 | convolution fusion | flops 6443368448 | bytes 16777216 | tf_op jit(solution)/shard_map/xmdc,cb->xmdb/dot_general | solution.py:14
  422.0 19.1 %fusion.5 = f32[256,32,256]{2,0,1:T(8,128)} fusion(f32[256,256]{1,0:T(8,128)S(1)} %copy.59, f32[256,256]{1,0:T(8,128)S(1)} %copy.58, pred[32]{0:T(512)(128)(4,1)S(1)} %dynamic-slice_compare_fusion, f32[32,256,256]{2,1,0:T(8,128)} %fusion.14, f32[32,256,256]{2,1,0:T(8,128)} %fusion.10, f32[32,256,256]{2,1,0:T(8,128)} %fusion.16, f32[32,256,256]{2,1,0:T(8,128)} %fusion.12), kind=kOutput, calls=%fused_computation.15 | convolution fusion | flops 6458048512 | bytes 42467360 | tf_op jit(solution)/shard_map/xmdb,da->xmab/dot_general | solution.py:14
  441.1 20.9 %fusion.20 = bf16[1,256,256,32]{2,1,3,0:T(8,128)(2,1)} fusion(f32[256,32,256]{2,0,1:T(8,128)} %fusion.5, f32[256,256]{1,0:T(8,128)S(1)} %copy.59, f32[256,256]{1,0:T(8,128)S(1)} %copy.58, pred[32]{0:T(512)(128)(4,1)S(1)} %dynamic-slice_compare_fusion, f32[32,256,256]{2,1,0:T(8,128)} %fusion.14, f32[32,256,256]{2,1,0:T(8,128)} %fusion.10, ...), kind=kOutput, calls=%fused_computation.39 | convolution fusion | flops 6464339968 | bytes 46661664 | tf_op jit(solution)/shard_map/xmdb,da->xmab/dot_general | solution.py:14
  473.1 9.2 %copy.75 = f32[1,8192,256]{1,2,0:T(8,128)} copy(f32[1,8192,256]{2,1,0:T(8,128)} %param.5) | data formatting | bytes 16777216 | tf_op args[0]
  482.3 83.3 %all-to-all-done.2 = bf16[1,256,256,32]{2,3,0,1:T(8,128)(2,1)} async-done(((bf16[1,256,256,32]{2,3,0,1:T(8,128)(2,1)}), bf16[1,256,256,32]{2,3,0,1:T(8,128)(2,1)}, u32[]{:S(2)}, u32[]{:S(2)}) %all-to-all-start.2) | async-done | bytes 4194336 | tf_op jit(solution)/shard_map/all_to_all | solution.py:107
  565.6 8.0 %copy.93 = f32[1,8,32,256,32]{3,2,4,1,0:T(8,128)} copy(bf16[1,8,32,256,32]{3,4,2,1,0:T(8,128)(2,1)} %bitcast.44) | data formatting | bytes 12582912 | tf_op jit(solution)/shard_map/convert_element_type | solution.py:109
  573.6 9.4 %reshape.154 = f32[1,8192,256]{1,2,0:T(8,128)} reshape(f32[1,32,256,8,32]{2,1,4,3,0:T(8,128)} %bitcast.139) | data formatting | bytes 16777216 | tf_op jit(solution)/shard_map/convert_element_type | solution.py:109
  583.0 16.1 %convert_bitcast_fusion.1 = bf16[1,8192,1024]{2,1,0:T(8,128)(2,1)} fusion(bf16[256,1024]{1,0:T(8,128)(2,1)S(1)} %copy-done, f32[1,8192,256]{1,2,0:T(8,128)} %reshape.154, f32[1,8192,256]{1,2,0:T(8,128)} %copy.75, f32[256]{0:T(256)S(1)} %copy-done.4), kind=kOutput, calls=%fused_computation.1 | convolution fusion | flops 4309647360 | bytes 34079744 | tf_op jit(solution)/shard_map/xtc,cj->xtj/dot_general | solution.py:116
  599.2 124.0 %reduce-scatter.2.cloned.1.call-done = bf16[1,8192,256]{2,1,0:T(8,128)(2,1)} async-done(((bf16[1,8192,1024]{2,1,0:T(8,128)(2,1)}), bf16[1,8192,256]{2,1,0:T(8,128)(2,1)}) %reduce-scatter.2.cloned.1.call-update) | async-done | bytes 4194320 | tf_op jit(solution)/shard_map/reduce_scatter | solution.py:117
  (33 shorter events, 47.3 us)
Async XLA Ops:
  6.5 576.5 %copy-start = (bf16[256,1024]{1,0:T(8,128)(2,1)S(1)}, bf16[256,1024]{1,0:T(8,128)(2,1)}, u32[]{:S(2)}) copy-start(bf16[256,1024]{1,0:T(8,128)(2,1)} %param.9) | copy-start | bytes 1572868
  20.3 100.6 %all-to-all-start = ((bf16[1,32,256,256]{2,1,0,3:T(8,128)(2,1)}), bf16[1,32,256,256]{2,1,0,3:T(8,128)(2,1)}, u32[]{:S(2)}, u32[]{:S(2)}) async-start(bf16[1,32,256,256]{2,1,0,3:T(8,128)(2,1)} %copy.55), calls=%async_computation | async-start | bytes 8388608 | tf_op jit(solution)/shard_map/all_to_all | solution.py:75
  44.5 83.6 %copy-start.5 = (s32[256]{0:T(256)S(1)}, s32[256]{0:T(256)}, u32[]{:S(2)}) copy-start(s32[256]{0:T(256)} %param.7) | copy-start | bytes 3076
  120.9 187.2 %all-to-all-start.1 = ((bf16[2,32,256,256]{2,1,0,3:T(8,128)(2,1)}), bf16[2,32,256,256]{2,1,0,3:T(8,128)(2,1)}, u32[]{:S(2)}, u32[]{:S(2)}) async-start(bf16[2,32,256,256]{2,1,0,3:T(8,128)(2,1)} %copy.62), calls=%async_computation.1 | async-start | bytes 16777216 | tf_op jit(solution)/shard_map/all_to_all | solution.py:78
  140.0 28.7 %copy-start.1 = (f32[256,32,256]{2,0,1:T(8,128)}, f32[256,32,256]{2,0,1:T(8,128)S(1)}, u32[]{:S(2)}) copy-start(f32[256,32,256]{2,0,1:T(8,128)S(1)} %fusion.58) | copy-start | bytes 25165828
  145.0 23.6 %copy-start.2 = (f32[256,32,256]{2,0,1:T(8,128)}, f32[256,32,256]{2,0,1:T(8,128)S(1)}, u32[]{:S(2)}) copy-start(f32[256,32,256]{2,0,1:T(8,128)S(1)} %fusion.50) | copy-start | bytes 25165828
  375.8 13.2 %copy-start.3 = (f32[1,32,256,256]{3,2,1,0:T(8,128)S(1)}, f32[1,32,256,256]{3,2,1,0:T(8,128)}, u32[]{:S(2)}) copy-start(f32[1,32,256,256]{3,2,1,0:T(8,128)} %get-tuple-element.6) | copy-start | bytes 25165828
  375.8 24.4 %slice-start = ((s8[8388608]{0:T(1024)(128)(4,1)}), s8[4194304]{0:T(1024)(128)(4,1)S(1)}, s32[]{:S(2)}) async-start(s8[8388608]{0:T(1024)(128)(4,1)} %bitcast.133), calls=%async_computation.5 | async-start | bytes 8388608
  389.0 11.2 %slice-start.1 = ((s8[8388608]{0:T(1024)(128)(4,1)}), s8[4194304]{0:T(1024)(128)(4,1)S(1)}, s32[]{:S(2)}) async-start(s8[8388608]{0:T(1024)(128)(4,1)} %bitcast.133), calls=%async_computation.6 | async-start | bytes 8388608
  468.5 97.0 %all-to-all-start.2 = ((bf16[1,256,256,32]{2,3,0,1:T(8,128)(2,1)}), bf16[1,256,256,32]{2,3,0,1:T(8,128)(2,1)}, u32[]{:S(2)}, u32[]{:S(2)}) async-start(bf16[1,256,256,32]{2,3,0,1:T(8,128)(2,1)} %copy.73), calls=%async_computation.2 | async-start | bytes 8388608 | tf_op jit(solution)/shard_map/all_to_all | solution.py:107
  473.1 250.1 %reduce-scatter.2.cloned.1.call-start = ((), (), s32[]{:S(2)}) async-start(), calls=%async_computation.4 | async-start | bytes 20971520 | tf_op jit(solution)/shard_map/reduce_scatter | solution.py:117
  573.6 9.4 %copy-start.4 = (f32[256]{0:T(256)S(1)}, f32[256]{0:T(256)}, u32[]{:S(2)}) copy-start(f32[256]{0:T(256)} %param.8) | copy-start | bytes 3076
Sparse Core Ops, SparseCore 0:
  599.3 123.8 reduce-scatter.1
where the time goes:
time: 748 us; the launch traced here: 737 us
  waiting for transfers between devices  409 us (55%)
  matrix products  177 us (24%)
  local copies, waits for them, and re-layouts  94.4 us (13%)
  other arithmetic  25.5 us (3%)
  starting transfers between devices  16.9 us (2%)
  between operations  14 us (2%)
    dot_general x12, matrix products, contract(): jnp.einsum(pattern, operand, matrix, precision=lax.Precision.HIGHEST, pre...  161 us
    all_to_all x1, waiting for transfers between devices, channel_plan(): lax.all_to_all(spectrum.astype(jnp.bfloat16), 'seq', split_axis=3, concat...  125 us
    reduce_scatter x1, waiting for transfers between devices, per_device(): lax.psum_scatter(partials.astype(jnp.bfloat16), 'ch', scatter_dimension=2...  124 us
    all_to_all x1, waiting for transfers between devices, channel_plan(): lax.all_to_all(convolved.astype(jnp.bfloat16), 'seq', split_axis=1, conca...  83.3 us
    all_to_all x1, waiting for transfers between devices, channel_plan(): lax.all_to_all(tiled.astype(jnp.bfloat16), 'seq', split_axis=3, concat_ax...  76.5 us
    unnamed x18, local copies, waits for them, and re-layouts  26 us
    transpose x1, local copies, waits for them, and re-layouts, channel_plan(): filters_first = jnp.transpose(filters, (0, 3, 1, 2))  17.8 us
    convert_element_type x2, local copies, waits for them, and re-layouts, channel_plan(): restored = lax.all_to_all(convolved.astype(jnp.bfloat16), 'seq', split_ax...  17.4 us
  transfers between devices with their start and end apart: 4, of which 4 were waited for; matrix products, arithmetic and copies ran while one was open for 11% of the time, Pallas kernels for 0%

commit v1 on v0

v1 whole, which is shorter than its diff:
```python
import math

import jax
import jax.numpy as jnp
from jax import lax
from jax.experimental import pallas as pl
from jax.experimental.pallas import tpu as pltpu
from jax.sharding import PartitionSpec as P


CHUNKS = 4


def phases(row_count, col_count, period):
    rows = jnp.arange(row_count, dtype=jnp.int32)
    cols = jnp.arange(col_count, dtype=jnp.int32)
    product = rows[:, None] * cols[None, :] % period
    angles = product.astype(jnp.float32) * (2.0 * math.pi / period)
    return jnp.cos(angles), jnp.sin(angles)


def tables(rows, columns):
    length = rows * columns
    rc, rs = phases(rows, rows, rows)
    cc, cs = phases(columns, columns, columns)
    first = jnp.concatenate([rc, -rs], 0)
    forward = jnp.concatenate(
        [jnp.concatenate([cc, -cs], 1), jnp.concatenate([cs, cc], 1)], 0
    )
    backward = jnp.concatenate(
        [jnp.concatenate([cc, cs], 1), jnp.concatenate([-cs, cc], 1)], 0
    )
    last = jnp.concatenate([rc, -rs], 1) / length
    twist_cos, twist_sin = phases(rows, columns, length)
    low = jnp.bfloat16
    return (
        first.astype(low),
        forward.astype(low),
        backward.astype(low),
        last.astype(low),
        twist_cos,
        twist_sin,
    )


def conv_kernel(
    mode_ref, x_ref, first_ref, forward_ref, backward_ref, last_ref, tc_ref, ts_ref, out_ref
):
    rows, columns = tc_ref.shape
    low = jnp.bfloat16

    def dot(a, b):
        return jnp.dot(a, b, preferred_element_type=jnp.float32)

    linear = mode_ref[pl.program_id(0)] == 1
    tc = jnp.where(linear, tc_ref[...], 1.0)
    ts = jnp.where(linear, ts_ref[...], 0.0)
    image = x_ref[:, 0, 0].reshape(rows, columns)
    y = dot(first_ref[...], image)
    yr, yi = y[:rows], y[rows:]
    y = jnp.concatenate(
        [(yr * tc + yi * ts).astype(low), (yi * tc - yr * ts).astype(low)], 1
    )
    z = dot(y, forward_ref[...])
    zr, zi = z[:, :columns], z[:, columns:]
    fr = x_ref[:, 1, 0].reshape(rows, columns).astype(jnp.float32)
    fi = x_ref[:, 2, 0].reshape(rows, columns).astype(jnp.float32)
    g = jnp.concatenate(
        [(zr * fr - zi * fi).astype(low), (zr * fi + zi * fr).astype(low)], 1
    )
    u = dot(g, backward_ref[...])
    ur, ui = u[:, :columns], u[:, columns:]
    v = jnp.concatenate(
        [(ur * tc - ui * ts).astype(low), (ur * ts + ui * tc).astype(low)], 0
    )
    out = dot(last_ref[...], v).astype(low)
    out_ref[:, 0] = out.reshape(out_ref.shape[0], out_ref.shape[2], columns)


def convolve(modes, received, consts):
    groups, planes, share, rows_local, columns = received.shape
    rows = groups * rows_local

    def whole(table):
        return pl.BlockSpec(table.shape, lambda c, m: (0,) * table.ndim)

    flops = share * 2 * 12 * rows * rows * columns
    return pl.pallas_call(
        conv_kernel,
        grid_spec=pltpu.PrefetchScalarGridSpec(
            num_scalar_prefetch=1,
            grid=(share,),
            in_specs=[
                pl.BlockSpec(
                    (groups, planes, 1, rows_local, columns), lambda c, m: (0, 0, c, 0, 0)
                )
            ]
            + [whole(t) for t in consts],
            out_specs=pl.BlockSpec(
                (groups, 1, rows_local, columns), lambda c, m: (0, c, 0, 0)
            ),
        ),
        out_shape=jax.ShapeDtypeStruct((groups, share, rows_local, columns), jnp.bfloat16),
        compiler_params=pltpu.CompilerParams(vmem_limit_bytes=24 * 1024 * 1024),
        cost_estimate=pl.CostEstimate(
            flops=flops, bytes_accessed=8 * share * rows * columns, transcendentals=0
        ),
    )(modes, received, *consts)


def per_device(signal, spectrum, channel_mode, skip_gain, out_weight):
    groups = lax.axis_size("seq")
    position = lax.axis_index("seq")
    channels_groups = lax.axis_size("ch")
    batches, local_len, owned = signal.shape
    rows_local, columns = spectrum.shape[1], spectrum.shape[2]
    rows = rows_local * groups
    chunk = owned // CHUNKS
    share = chunk // groups
    low = jnp.bfloat16
    consts = tables(rows, columns)
    weights = lax.all_to_all(out_weight, "ch", split_axis=1, concat_axis=0, tiled=True)
    out_cols = weights.shape[1]

    def pack(j, sig, spec):
        lo = j * chunk
        sig = sig[0, :, lo : lo + chunk].reshape(1, rows_local, columns, chunk)
        both = jnp.concatenate([sig.astype(low), spec[..., lo : lo + chunk].astype(low)], 0)
        both = both.reshape(3, rows_local, columns, groups, share)
        return jnp.transpose(both, (3, 0, 4, 1, 2))

    def send(j):
        return lax.all_to_all(packed[j], "seq", split_axis=0, concat_axis=0, tiled=True)

    def finish(j, back, total):
        gain = skip_gain[j * chunk : (j + 1) * chunk].reshape(groups, share, 1, 1)
        hidden = (
            back.astype(jnp.float32) + gain * packed[j][:, 0].astype(jnp.float32)
        ).astype(low)
        hidden = hidden.reshape(chunk, rows_local, columns)
        spread = lax.all_gather(hidden, "ch", axis=0, tiled=False)
        spread = spread.reshape(channels_groups * chunk, rows_local, columns)
        part = jnp.einsum(
            "cae,cj->aej",
            spread,
            weights[:, j].reshape(channels_groups * chunk, out_cols),
            preferred_element_type=jnp.float32,
        )
        return part if total is None else lax.optimization_barrier(total) + part

    packed = []
    sig, spec = signal, spectrum
    for j in range(CHUNKS):
        block = pack(j, sig, spec)
        if j == 1:
            block, weights = lax.optimization_barrier((block, weights))
        sig, spec, block = lax.optimization_barrier((sig, spec, block))
        packed.append(block)
    weights = weights.reshape(channels_groups, CHUNKS, chunk, out_cols)

    total, back = None, None
    received = send(0)
    for j in range(CHUNKS):
        modes = lax.dynamic_slice_in_dim(
            channel_mode, j * chunk + position * share, share
        )
        following = None
        if j + 1 < CHUNKS:
            if back is not None:
                packed[j + 1], back = lax.optimization_barrier((packed[j + 1], back))
            else:
                packed[j + 1], received = lax.optimization_barrier((packed[j + 1], received))
            following = send(j + 1)
        conv = convolve(modes, received, consts)
        if following is not None:
            conv, following = lax.optimization_barrier((conv, following))
        elif back is not None:
            conv, back = lax.optimization_barrier((conv, back))
        if back is not None:
            total = finish(j - 1, back, total)
        back = lax.all_to_all(conv, "seq", split_axis=0, concat_axis=0, tiled=True)
        received = following
    total = finish(CHUNKS - 1, back, total)
    return total.reshape(batches, local_len, out_cols)


def solution(mesh):
    placed = (P(None, "seq", "ch"), P(None, "seq", None, "ch"), P("ch"), P("ch"), P("ch", None))
    return jax.shard_map(
        per_device, mesh=mesh, in_specs=placed, out_specs=P(None, "seq", "ch"), check_vma=False
    )
```

time: 748 us -> 535 us (0.72)
  waiting for transfers between devices: 409 us -> 235 us
  matrix products: 177 us -> 51.7 us
  Pallas kernels: 0 us -> 37.2 us
  local copies, waits for them, and re-layouts: 94.4 us -> 122 us
  starting transfers between devices: 16.9 us -> 44.2 us
    dot_general x13 -> x4, matrix products: 177 us -> 51.7 us  [finish(): jnp.einsum('cae,cj->aej', spread, weights[:, j].reshape(channels_groups *...]
    reduce_scatter x1 -> x0, waiting for transfers between devices: 124 us -> none  [per_device(): lax.psum_scatter(partials.astype(jnp.bfloat16), 'ch', scatter_dimension=2...]
    all_to_all x3 -> x9, waiting for transfers between devices: 285 us -> 234 us  [the longest x4 197 us: send(): lax.all_to_all(packed[j], 'seq', split_axis=0, concat_axis=0, tiled=True)]
    optimization_barrier x0 -> x3, local copies, waits for them, and re-layouts: none -> 41.6 us  [per_device(): sig, spec, block = lax.optimization_barrier((sig, spec, block))]
    pallas_call x0 -> x4, Pallas kernels: none -> 37.2 us  [convolve(): pl.pallas_call(conv_kernel, grid_spec=pltpu.PrefetchScalarGridSpec(num_sc...]
    convert_element_type x4 -> x0, local copies, waits for them, and re-layouts: 31.9 us -> none  [the longest x2 17.4 us: channel_plan(): restored = lax.all_to_all(convolved.astype(jnp.bfloat16), 'seq', split_ax...]
    slice x0 -> x11, local copies, waits for them, and re-layouts: none -> 31.2 us  [the longest x8 24.9 us: pack(): sig = sig[0, :, lo:lo + chunk].reshape(1, rows_local, columns, chunk)]
    all_to_all x3 -> x9, starting transfers between devices: 16.8 us -> 43.8 us  [the longest x4 22.6 us: send(): lax.all_to_all(packed[j], 'seq', split_axis=0, concat_axis=0, tiled=True)]
  transfers between devices with their start and end apart: 4 -> 13, of which waited for: 4 -> 7; matrix products, arithmetic and copies ran while one was open for 11% -> 30% of each run, Pallas kernels for 0% -> 7%
where the time goes in v1:
time: 535 us; the launch traced here: 527 us
  waiting for transfers between devices  235 us (44%)
  local copies, waits for them, and re-layouts  122 us (23%)
  matrix products  51.7 us (10%)
  starting transfers between devices  44.2 us (8%)
  Pallas kernels  37.2 us (7%)
  other arithmetic  23.3 us (4%)
  between operations  13.7 us (3%)
    all_to_all x4, waiting for transfers between devices, send(): lax.all_to_all(packed[j], 'seq', split_axis=0, concat_axis=0, tiled=True)  197 us
    dot_general x4, matrix products, finish(): jnp.einsum('cae,cj->aej', spread, weights[:, j].reshape(channels_groups *...  51.7 us
    optimization_barrier x3, local copies, waits for them, and re-layouts, per_device(): sig, spec, block = lax.optimization_barrier((sig, spec, block))  41.6 us
    pallas_call x4, Pallas kernels, convolve(): pl.pallas_call(conv_kernel, grid_spec=pltpu.PrefetchScalarGridSpec(num_sc...  37.2 us
    all_to_all x4, waiting for transfers between devices, per_device(): back = lax.all_to_all(conv, 'seq', split_axis=0, concat_axis=0, tiled=True)  37.1 us
    unnamed x66, local copies, waits for them, and re-layouts  32.8 us
    slice x8, local copies, waits for them, and re-layouts, pack(): sig = sig[0, :, lo:lo + chunk].reshape(1, rows_local, columns, chunk)  24.9 us
    all_to_all x4, starting transfers between devices, send(): lax.all_to_all(packed[j], 'seq', split_axis=0, concat_axis=0, tiled=True)  22.6 us
  transfers between devices with their start and end apart: 13, of which 7 were waited for; matrix products, arithmetic and copies ran while one was open for 30% of the time, Pallas kernels for 7%

profile of v1, /device:TPU:0, one launch (start us, length us, event | category | flops | bytes accessed | tf_op | source)
XLA Modules:
  0.0 527.0 jit_solution(5271965859885302919)
XLA Ops:
  12.8 6.1 %slice.121 = bf16[2,32,256,64]{3,2,1,0:T(8,128)(2,1)} slice(f32[2,32,256,256]{3,2,1,0:T(8,128)} %param.6), slice={[0:2], [0:32], [0:256], [0:64]} | slice | bytes 4194304 | tf_op jit(solution)/shard_map/slice | solution.py:128
  19.0 4.8 copy.66
  34.3 7.2 %all-to-all-start.1 = ((bf16[8,3,8,32,256]{4,3,2,1,0:T(8,128)(2,1)}), bf16[8,3,8,32,256]{4,3,2,1,0:T(8,128)(2,1)S(1)}, u32[]{:S(2)}, u32[]{:S(2)}) async-start(bf16[8,3,8,32,256]{4,3,2,1,0:T(8,128)(2,1)} %maximum_bitcast_fusion), calls=%async_computation.1 | async-start | bytes 6291456 | tf_op jit(solution)/shard_map/all_to_all | solution.py:133
  41.5 13.9 %copy.52 = bf16[2,32,256,256]{2,3,1,0:T(8,128)(2,1)} copy(f32[2,32,256,256]{3,2,1,0:T(8,128)} %param.6) | data formatting | bytes 25165824 | tf_op jit(solution)/shard_map/optimization_barrier | solution.py:157
  72.4 40.5 %all-to-all-done.1.x_ref = bf16[8,3,8,32,256]{4,3,2,1,0:T(8,128)(2,1)S(1)} async-done(((bf16[8,3,8,32,256]{4,3,2,1,0:T(8,128)(2,1)}), bf16[8,3,8,32,256]{4,3,2,1,0:T(8,128)(2,1)S(1)}, u32[]{:S(2)}, u32[]{:S(2)}) %all-to-all-start.1) | async-done | bytes 3145760 | tf_op jit(solution)/shard_map/all_to_all | solution.py:133
  123.7 9.0 %shard_map.55 = bf16[8,8,32,256]{3,2,1,0:T(8,128)(2,1)S(1)} custom-call(s32[8]{0:T(128)S(1)} %get-tuple-element.69.mode_ref, bf16[8,3,8,32,256]{4,3,2,1,0:T(8,128)(2,1)S(1)} %copy-done.1, bf16[512,256]{1,0:T(8,128)(2,1)S(1)} %pad_maximum_fusion.3.first_ref, bf16[512,512]{1,0:T(8,128)(2,1)S(1)} %get-tuple-element.62.forward_ref, ...), custom_call_target="tpu_custom_call" | custom-call | flops 3221225472 | bytes 4194304 | tf_op jit(solution)/shard_map/pallas_call | solution.py:88
  135.3 54.0 %all-to-all-done.2.x_ref = bf16[8,3,8,32,256]{4,3,2,1,0:T(8,128)(2,1)S(1)} async-done(((bf16[8,3,8,32,256]{4,3,2,1,0:T(8,128)(2,1)}), bf16[8,3,8,32,256]{4,3,2,1,0:T(8,128)(2,1)S(1)}, u32[]{:S(2)}, u32[]{:S(2)}) %all-to-all-start.2) | async-done | bytes 3145760 | tf_op jit(solution)/shard_map/all_to_all | solution.py:133
  193.6 13.9 %copy.57 = bf16[2,32,256,256]{2,3,1,0:T(8,128)(2,1)} copy(f32[2,32,256,256]{3,2,1,0:T(8,128)} %param.6) | data formatting | bytes 25165824 | tf_op jit(solution)/shard_map/optimization_barrier | solution.py:157
  222.0 6.0 %all-to-all-start.4 = ((bf16[8,3,8,32,256]{4,3,2,1,0:T(8,128)(2,1)}), bf16[8,3,8,32,256]{4,3,2,1,0:T(8,128)(2,1)}, u32[]{:S(2)}, u32[]{:S(2)}) async-start(bf16[8,3,8,32,256]{4,3,2,1,0:T(8,128)(2,1)} %maximum_bitcast_fusion.2), calls=%async_computation.4 | async-start | bytes 6291456 | tf_op jit(solution)/shard_map/all_to_all | solution.py:133
  236.1 8.9 %shard_map.56 = bf16[8,8,32,256]{3,2,1,0:T(8,128)(2,1)S(1)} custom-call(s32[8]{0:T(128)S(1)} %get-tuple-element.68.mode_ref, bf16[8,3,8,32,256]{4,3,2,1,0:T(8,128)(2,1)S(1)} %all-to-all-done.2.x_ref, bf16[512,256]{1,0:T(8,128)(2,1)S(1)} %copy-done.14, bf16[512,512]{1,0:T(8,128)(2,1)S(1)} %copy-done.10, bf16[512,512]{1,0:T(8,128)(2,1)S(1)} %copy-done.6, ...), custom_call_target="tpu_custom_call" | custom-call | flops 3221225472 | bytes 4194304 | tf_op jit(solution)/shard_map/pallas_call | solution.py:88
  246.0 51.9 %all-to-all-done.4.x_ref = bf16[8,3,8,32,256]{4,3,2,1,0:T(8,128)(2,1)} async-done(((bf16[8,3,8,32,256]{4,3,2,1,0:T(8,128)(2,1)}), bf16[8,3,8,32,256]{4,3,2,1,0:T(8,128)(2,1)}, u32[]{:S(2)}, u32[]{:S(2)}) %all-to-all-start.4) | async-done | bytes 3145760 | tf_op jit(solution)/shard_map/all_to_all | solution.py:133
  297.9 4.8 all-to-all-start.5
  302.7 13.9 %copy.61 = bf16[2,32,256,256]{2,3,1,0:T(8,128)(2,1)} copy(f32[2,32,256,256]{3,2,1,0:T(8,128)} %param.6) | data formatting | bytes 25165824 | tf_op jit(solution)/shard_map/optimization_barrier | solution.py:157
  328.3 5.4 %all-to-all-start.6 = ((bf16[8,3,8,32,256]{4,3,2,1,0:T(8,128)(2,1)}), bf16[8,3,8,32,256]{4,3,2,1,0:T(8,128)(2,1)S(1)}, u32[]{:S(2)}, u32[]{:S(2)}) async-start(bf16[8,3,8,32,256]{4,3,2,1,0:T(8,128)(2,1)} %maximum_bitcast_fusion.3), calls=%async_computation.6 | async-start | bytes 6291456 | tf_op jit(solution)/shard_map/all_to_all | solution.py:133
  341.7 9.8 %shard_map.57 = bf16[8,8,32,256]{3,2,1,0:T(8,128)(2,1)S(1)} custom-call(s32[8]{0:T(128)S(1)} %get-tuple-element.67.mode_ref, bf16[8,3,8,32,256]{4,3,2,1,0:T(8,128)(2,1)} %all-to-all-done.4.x_ref, bf16[512,256]{1,0:T(8,128)(2,1)S(1)} %copy-done.15, bf16[512,512]{1,0:T(8,128)(2,1)S(1)} %copy-done.11, bf16[512,512]{1,0:T(8,128)(2,1)S(1)} %copy-done.7, ...), custom_call_target="tpu_custom_call" | custom-call | flops 3221225472 | bytes 4194304 | tf_op jit(solution)/shard_map/pallas_call | solution.py:88
  352.5 51.0 %all-to-all-done.6.x_ref = bf16[8,3,8,32,256]{4,3,2,1,0:T(8,128)(2,1)S(1)} async-done(((bf16[8,3,8,32,256]{4,3,2,1,0:T(8,128)(2,1)}), bf16[8,3,8,32,256]{4,3,2,1,0:T(8,128)(2,1)S(1)}, u32[]{:S(2)}, u32[]{:S(2)}) %all-to-all-start.6) | async-done | bytes 3145760 | tf_op jit(solution)/shard_map/all_to_all | solution.py:133
  403.5 4.2 all-to-all-start.7
  412.8 9.5 %shard_map.58 = bf16[8,8,32,256]{3,2,1,0:T(8,128)(2,1)} custom-call(s32[8]{0:T(128)S(1)} %get-tuple-element.70.mode_ref, bf16[8,3,8,32,256]{4,3,2,1,0:T(8,128)(2,1)S(1)} %all-to-all-done.6.x_ref, bf16[512,256]{1,0:T(8,128)(2,1)S(1)} %copy-done.16, bf16[512,512]{1,0:T(8,128)(2,1)S(1)} %copy-done.12, bf16[512,512]{1,0:T(8,128)(2,1)S(1)} %copy-done.8, ...), custom_call_target="tpu_custom_call" | custom-call | flops 3221225472 | bytes 4194304 | tf_op jit(solution)/shard_map/pallas_call | solution.py:88
  422.4 11.0 %all-to-all-done.7 = bf16[8,8,32,256]{3,2,1,0:T(8,128)(2,1)} async-done(((bf16[8,8,32,256]{3,2,1,0:T(8,128)(2,1)}), bf16[8,8,32,256]{3,2,1,0:T(8,128)(2,1)}, u32[]{:S(2)}, u32[]{:S(2)}) %all-to-all-start.7) | async-done | bytes 1048608 | tf_op jit(solution)/shard_map/all_to_all | solution.py:181
  440.3 25.5 %all-to-all-done.8 = bf16[8,8,32,256]{3,2,1,0:T(8,128)(2,1)S(1)} async-done(((bf16[8,8,32,256]{3,2,1,0:T(8,128)(2,1)}), bf16[8,8,32,256]{3,2,1,0:T(8,128)(2,1)S(1)}, u32[]{:S(2)}, u32[]{:S(2)}) %all-to-all-start.8) | async-done | bytes 1048608 | tf_op jit(solution)/shard_map/all_to_all | solution.py:181
  468.5 10.9 %fusion.6 = f32[32,256,256]{2,1,0:T(8,128)} fusion(bf16[256,256,1]{1,0,2:T(8,128)(2,1)S(1)} %bitcast.111, bf16[256,32,256]{2,1,0:T(8,128)(2,1)} %bitcast.91), kind=kOutput, calls=%fused_computation.13 | convolution fusion | flops 1073741824 | bytes 12713984 | tf_op jit(solution)/shard_map/cae,cj->aej/dot_general | solution.py:143
  479.4 13.9 %fusion.8 = f32[32,256,256]{2,1,0:T(8,128)} fusion(f32[32,256,256]{2,1,0:T(8,128)} %fusion.6, bf16[256,256,1]{1,0,2:T(8,128)(2,1)S(1)} %bitcast.110, bf16[256,32,256]{2,1,0:T(8,128)(2,1)} %bitcast.92), kind=kOutput, calls=%fused_computation.15 | convolution fusion | flops 1075838976 | bytes 21102592 | tf_op jit(solution)/shard_map/cae,cj->aej/dot_general | solution.py:143
  493.3 13.6 %fusion.11 = f32[32,256,256]{2,1,0:T(8,128)} fusion(f32[32,256,256]{2,1,0:T(8,128)} %fusion.8, bf16[256,256,1]{1,0,2:T(8,128)(2,1)S(1)} %bitcast.109, bf16[256,32,256]{2,1,0:T(8,128)(2,1)} %bitcast.93), kind=kOutput, calls=%fused_computation.16 | convolution fusion | flops 1075838976 | bytes 21102592 | tf_op jit(solution)/shard_map/cae,cj->aej/dot_general | solution.py:143
  506.9 13.3 %fusion.14 = f32[32,256,256]{2,1,0:T(8,128)} fusion(f32[32,256,256]{2,1,0:T(8,128)} %fusion.11, bf16[256,256,1]{1,0,2:T(8,128)(2,1)S(1)} %bitcast.108, bf16[256,32,256]{2,1,0:T(8,128)(2,1)} %bitcast.94), kind=kOutput, calls=%fused_computation.17 | convolution fusion | flops 1075838976 | bytes 21102592 | tf_op jit(solution)/shard_map/cae,cj->aej/dot_general | solution.py:143
  (123 shorter events, 110.2 us)
Async XLA Ops:
  8.6 25.7 %all-to-all-start = ((bf16[256,4,256]{0,2,1:T(8,128)(2,1)}), bf16[256,4,256]{0,2,1:T(8,128)(2,1)}, u32[]{:S(2)}, u32[]{:S(2)}) async-start(bf16[256,4,256]{0,2,1:T(8,128)(2,1)} %bitcast.4), calls=%async_computation | async-start | bytes 1048576 | tf_op jit(solution)/shard_map/all_to_all | solution.py:122
  34.3 78.6 %all-to-all-start.1 = ((bf16[8,3,8,32,256]{4,3,2,1,0:T(8,128)(2,1)}), bf16[8,3,8,32,256]{4,3,2,1,0:T(8,128)(2,1)S(1)}, u32[]{:S(2)}, u32[]{:S(2)}) async-start(bf16[8,3,8,32,256]{4,3,2,1,0:T(8,128)(2,1)} %maximum_bitcast_fusion), calls=%async_computation.1 | async-start | bytes 6291456 | tf_op jit(solution)/shard_map/all_to_all | solution.py:133
  66.5 1.9 copy-start.25
  72.4 46.1 %copy-start.28 = (s32[256]{0:T(256)S(1)}, s32[256]{0:T(256)}, u32[]{:S(2)}) copy-start(s32[256]{0:T(256)} %param.7) | copy-start | bytes 3076
  112.8 1.7 copy-start
  114.5 74.8 %all-to-all-start.2 = ((bf16[8,3,8,32,256]{4,3,2,1,0:T(8,128)(2,1)}), bf16[8,3,8,32,256]{4,3,2,1,0:T(8,128)(2,1)S(1)}, u32[]{:S(2)}, u32[]{:S(2)}) async-start(bf16[8,3,8,32,256]{4,3,2,1,0:T(8,128)(2,1)} %maximum_bitcast_fusion.1), calls=%async_computation.2 | async-start | bytes 6291456 | tf_op jit(solution)/shard_map/all_to_all | solution.py:133
  118.5 5.2 copy-start.1
  121.8 1.1 copy-start.13
  189.3 32.6 %all-to-all-start.3 = ((bf16[8,8,32,256]{3,2,1,0:T(8,128)(2,1)}), bf16[8,8,32,256]{3,2,1,0:T(8,128)(2,1)}, u32[]{:S(2)}, u32[]{:S(2)}) async-start(bf16[8,8,32,256]{3,2,1,0:T(8,128)(2,1)} %copy-done.3), calls=%async_computation.3 | async-start | bytes 2097152 | tf_op jit(solution)/shard_map/all_to_all | solution.py:181
  218.2 1.9 copy-start.26
  222.0 6.1 %copy-start.29 = (f32[256]{0:T(256)S(1)}, f32[256]{0:T(256)}, u32[]{:S(2)}) copy-start(f32[256]{0:T(256)} %param.8) | copy-start | bytes 3076
  222.0 76.0 %all-to-all-start.4 = ((bf16[8,3,8,32,256]{4,3,2,1,0:T(8,128)(2,1)}), bf16[8,3,8,32,256]{4,3,2,1,0:T(8,128)(2,1)}, u32[]{:S(2)}, u32[]{:S(2)}) async-start(bf16[8,3,8,32,256]{4,3,2,1,0:T(8,128)(2,1)} %maximum_bitcast_fusion.2), calls=%async_computation.4 | async-start | bytes 6291456 | tf_op jit(solution)/shard_map/all_to_all | solution.py:133
  228.0 240.5 %all-gather.5.cloned.1.call-start = ((), (), s32[]{:S(2)}) async-start(), calls=%async_computation.9 | async-start | bytes 5242880 | tf_op jit(solution)/shard_map/all_gather | solution.py:141
  231.2 1.0 copy-start.6
  297.9 30.4 %all-to-all-start.5 = ((bf16[8,8,32,256]{3,2,1,0:T(8,128)(2,1)}), bf16[8,8,32,256]{3,2,1,0:T(8,128)(2,1)}, u32[]{:S(2)}, u32[]{:S(2)}) async-start(bf16[8,8,32,256]{3,2,1,0:T(8,128)(2,1)} %copy-done.4), calls=%async_computation.5 | async-start | bytes 2097152 | tf_op jit(solution)/shard_map/all_to_all | solution.py:181
  328.3 75.2 %all-to-all-start.6 = ((bf16[8,3,8,32,256]{4,3,2,1,0:T(8,128)(2,1)}), bf16[8,3,8,32,256]{4,3,2,1,0:T(8,128)(2,1)S(1)}, u32[]{:S(2)}, u32[]{:S(2)}) async-start(bf16[8,3,8,32,256]{4,3,2,1,0:T(8,128)(2,1)} %maximum_bitcast_fusion.3), calls=%async_computation.6 | async-start | bytes 6291456 | tf_op jit(solution)/shard_map/all_to_all | solution.py:133
  333.7 145.7 %all-gather.7.cloned.1.call-start = ((), (), s32[]{:S(2)}) async-start(), calls=%async_computation.10 | async-start | bytes 5242880 | tf_op jit(solution)/shard_map/all_gather | solution.py:141
  336.8 1.0 copy-start.7
  403.5 29.8 %all-to-all-start.7 = ((bf16[8,8,32,256]{3,2,1,0:T(8,128)(2,1)}), bf16[8,8,32,256]{3,2,1,0:T(8,128)(2,1)}, u32[]{:S(2)}, u32[]{:S(2)}) async-start(bf16[8,8,32,256]{3,2,1,0:T(8,128)(2,1)} %copy-done.2), calls=%async_computation.7 | async-start | bytes 2097152 | tf_op jit(solution)/shard_map/all_to_all | solution.py:181
  407.8 85.6 %all-gather.9.cloned.1.call-start = ((), (), s32[]{:S(2)}) async-start(), calls=%async_computation.11 | async-start | bytes 5242880 | tf_op jit(solution)/shard_map/all_gather | solution.py:141
  407.9 1.0 copy-start.8
  436.3 32.2 %copy-start.27 = (bf16[4,256,256]{2,1,0:T(8,128)(2,1)S(1)}, bf16[4,256,256]{2,1,0:T(8,128)(2,1)}, u32[]{:S(2)}) copy-start(bf16[4,256,256]{2,1,0:T(8,128)(2,1)} %copy.55) | copy-start | bytes 1572868
  436.3 29.5 %all-to-all-start.8 = ((bf16[8,8,32,256]{3,2,1,0:T(8,128)(2,1)}), bf16[8,8,32,256]{3,2,1,0:T(8,128)(2,1)S(1)}, u32[]{:S(2)}, u32[]{:S(2)}) async-start(bf16[8,8,32,256]{3,2,1,0:T(8,128)(2,1)} %shard_map.58), calls=%async_computation.8 | async-start | bytes 2097152 | tf_op jit(solution)/shard_map/all_to_all | solution.py:181
  440.0 67.0 %all-gather.11.cloned.1.call-start = ((), (), s32[]{:S(2)}) async-start(), calls=%async_computation.12 | async-start | bytes 5242880 | tf_op jit(solution)/shard_map/all_gather | solution.py:141
  (19 other events, 17.8 us)
Sparse Core Ops, SparseCore 0:
  231.3 36.0 all-gather.4
  336.9 35.9 all-gather.6
  436.4 33.4 all-gather.8
  471.3 34.3 all-gather.10
